TPU v7x, 32 devices: a whole 2x2x4 slice. The times are simulated.
32 devices in a mesh: space: 16 (over z, y, core), tm: 2 (over x).
Axes of the slice: x: 2, y: 2, z: 4, core: 2. Of those that a mesh axis runs over, the one named last changes fastest.
Arguments:
- solutions: bfloat16 [2, 12, 8192, 128], P('tm', None, 'space'), may hold values from -6 to 6
- noise: int32 [2, 64, 12, 8192], P('tm', None, None, 'space'), may hold values from 0 to 3
- momenta: int32 [27, 3], replicated, may hold values from -2 to 2
- pairs: int32 [16, 2], P('tm'), may hold values from 0 to 1
Outputs:
- mesons: float32 [2, 2, 27, 64, 64], P('tm', None, None, 'space')
- correlators: float32 [16, 2, 27], P('tm')
All inputs are finite; a program needn't handle non-finite values.
Results may differ from a plain program's by a relative error of at most 0.002.
Values sent between devices are 32-bit elements; how exact they have to be, the bound alone decides.
A program may use at most 64 MiB of HBM per device.

v0:
```python
import functools
import math

import jax
import jax.numpy as jnp
from jax import lax
from jax.experimental import pallas as pl
from jax.experimental.pallas import tpu as pltpu
from jax.sharding import PartitionSpec as P

EXTENT = 48
QC = 4
GROUP = 2
MESH = pl.DeviceIdType.MESH


def wrap(value):
    return jnp.floor((value + 0.5) * jnp.float32(1.0 / EXTENT))


def column(ref, row):
    size = ref.shape[1]
    here = lax.broadcasted_iota(jnp.int32, (size, size), 0)
    there = lax.broadcasted_iota(jnp.int32, (size, size), 1)
    line = jnp.broadcast_to(ref[row:row + 1, :].astype(jnp.float32), (size, size))
    return jnp.sum(jnp.where(here == there, line, jnp.float32(0.0)), axis=1, keepdims=True)


def phases(mom_ref, offset, sites):
    moms = mom_ref.shape[1]
    glob = (lax.broadcasted_iota(jnp.int32, (moms, sites), 1) + offset).astype(jnp.float32)
    line = wrap(glob)
    plane = wrap(line)
    xx = glob - line * EXTENT
    yy = line - plane * EXTENT
    dot = column(mom_ref, 0) * xx + column(mom_ref, 1) * yy + column(mom_ref, 2) * plane
    angle = (dot - wrap(dot) * EXTENT) * jnp.float32(2.0 * math.pi / EXTENT)
    base_re = jnp.cos(angle).astype(jnp.bfloat16).astype(jnp.float32)
    base_im = (-jnp.sin(angle)).astype(jnp.bfloat16).astype(jnp.float32)
    return base_re, base_im


def kernel(dims, mom_ref, pair_ref, noise_hbm, sol_hbm, mes_ref, tr_ref,
           base_ref, raw, sol, nre, nim, acc, sbuf, hbuf, qbuf, rcore, ry, rz, xb, ps,
           in_sem, cs, cr, ys, yr, zs, zr, xs, xr, pss, psr):
    nspace, nslices, nchunks, rows, nvec, spincol, scale = dims
    nz = nspace // 4
    me = lax.axis_index("space")
    slice_id = lax.axis_index("tm")
    core = lax.rem(me, 2)
    yy = lax.rem(me // 2, 2)
    zz = me // 4

    barrier = pltpu.get_barrier_semaphore()
    for o in range(1, nspace):
        pl.semaphore_signal(barrier, inc=1, device_id={"space": lax.rem(me + o, nspace)}, device_id_type=MESH)
    for o in range(1, nslices):
        pl.semaphore_signal(barrier, inc=1, device_id={"tm": lax.rem(slice_id + o, nslices)}, device_id_type=MESH)

    noise_copy = pltpu.make_async_copy(noise_hbm, raw, in_sem.at[0])
    sol_copy = pltpu.make_async_copy(sol_hbm, sol, in_sem.at[1])
    noise_copy.start()
    sol_copy.start()
    moms = mom_ref.shape[1]
    base_re, base_im = phases(mom_ref, me * sol.shape[1], sol.shape[1])
    base_ref[...] = jnp.zeros_like(base_ref)
    base_ref[0, :moms] = base_re
    base_ref[1, :moms] = base_im
    noise_copy.wait()

    def turn(a, carry):
        k = raw[a]
        one = jnp.float32(1.0)
        zero = jnp.float32(0.0)
        re = jnp.where(k == 0, one, jnp.where(k == 2, -one, zero))
        im = jnp.where(k == 3, one, jnp.where(k == 1, -one, zero))
        nre[a] = re.astype(jnp.bfloat16)
        nim[a] = im.astype(jnp.bfloat16)
        return carry

    for a in range(spincol):
        turn(a, 0)
    sol_copy.wait()

    lane = lax.broadcasted_iota(jnp.int32, (QC * nvec, 2 * nvec), 1)
    sign = jnp.where(lane < nvec, jnp.float32(-1.0), jnp.float32(1.0))
    lane_r = lax.broadcasted_iota(jnp.int32, (nchunks * QC * rows, 2 * nvec), 1)
    sign_r = jnp.where(lane_r < nvec, jnp.float32(-1.0), jnp.float32(1.0))

    def compute(c):
        acc[...] = jnp.zeros_like(acc)
        sites = base_ref.shape[2]

        def body(step, carry):
            columns = []
            for k in range(GROUP):
                a = step * GROUP + k
                wre, wim = [], []
                n_r, n_i = nre[a], nim[a]
                for qq in range(QC):
                    q = c * QC + qq
                    br = jnp.broadcast_to(base_ref[0, pl.ds(q, 1), :].astype(jnp.bfloat16), (nvec, sites))
                    bi = jnp.broadcast_to(base_ref[1, pl.ds(q, 1), :].astype(jnp.bfloat16), (nvec, sites))
                    wre.append(n_r * br - n_i * bi)
                    wim.append(n_r * bi + n_i * br)
                columns.append(jnp.concatenate(wre + wim, axis=0))
            w = jnp.concatenate(columns, axis=1)
            v = sol[pl.ds(step * GROUP, GROUP)].reshape(GROUP * sites, 2 * nvec)
            acc[...] += jnp.dot(w, v, preferred_element_type=jnp.float32)
            return carry

        lax.fori_loop(0, spincol // GROUP, body, 0)
        left = acc[: QC * nvec, :]
        right = acc[QC * nvec:, :]
        field = left + pltpu.roll(right, nvec, 1) * sign
        for qq in range(QC):
            for d in range(nspace):
                first = qq * nvec + d * rows
                sbuf[c, d % 2, (d // 2) % 2, d // 4, qq * rows:(qq + 1) * rows, :] = field[first:first + rows, :]

    def remote(src, dst, ssem, rsem, where):
        return pltpu.make_async_remote_copy(src_ref=src, dst_ref=dst, send_sem=ssem, recv_sem=rsem,
                                            device_id=where, device_id_type=MESH)

    core_peer = {"space": me + 1 - 2 * core}
    y_peer = {"space": me + 2 - 4 * yy}

    def core_copy(c):
        return remote(sbuf.at[c, 1 - core], rcore.at[c], cs.at[c], cr.at[c], core_peer)

    def y_copy(c):
        return remote(hbuf.at[c, 1 - yy], ry.at[c], ys.at[c], yr.at[c], y_peer)

    def z_copy(c, o):
        to = lax.rem(zz + o, nz)
        return remote(qbuf.at[c, to], rz.at[c, o - 1], zs.at[c, o - 1], zr.at[c, o - 1],
                      {"space": to * 4 + yy * 2 + core})

    def x_copy(c, o):
        return remote(xb.at[slice_id, c], xb.at[slice_id, c], xs.at[c, o - 1], xr.at[c, o - 1],
                      {"tm": lax.rem(slice_id + o, nslices)})

    def p_copy(o):
        return remote(ps.at[me], ps.at[me], pss.at[o - 1], psr.at[o - 1],
                      {"space": lax.rem(me + o, nspace)})

    for step in range(nchunks + 3):
        c = step
        if c < nchunks:
            compute(c)
            if c == 0:
                pl.semaphore_wait(barrier, nspace - 1 + nslices - 1)
            core_copy(c).start()
        c = step - 1
        if 0 <= c < nchunks:
            core_copy(c).wait_recv()
            hbuf[c, 1 - yy] = sbuf[c, core, 1 - yy] + rcore[c, 1 - yy]
            y_copy(c).start()
            hbuf[c, yy] = sbuf[c, core, yy] + rcore[c, yy]
        c = step - 2
        if 0 <= c < nchunks:
            y_copy(c).wait_recv()
            qbuf[c] = hbuf[c, yy] + ry[c]
            for o in range(1, nz):
                z_copy(c, o).start()
        c = step - 3
        if 0 <= c < nchunks:
            for o in range(1, nz):
                z_copy(c, o).wait_recv()
            total = qbuf[c, zz]
            for o in range(1, nz):
                total = total + rz[c, o - 1]
            total = total * jnp.float32(scale)
            xb[slice_id, c] = total
            for qq in range(min(QC, moms - c * QC)):
                part = total[qq * rows:(qq + 1) * rows, :]
                mes_ref[0, c * QC + qq] = part[:, :nvec]
                mes_ref[1, c * QC + qq] = part[:, nvec:]
            for o in range(1, nslices):
                x_copy(c, o).start()

    for c in range(nchunks):
        for o in range(1, nslices):
            x_copy(c, o).wait_recv()

    lq = nchunks * QC * rows
    trows = ps.shape[1]
    rowid = lax.broadcasted_iota(jnp.int32, (trows, 2 * nvec), 0)
    found = jnp.zeros((trows, lq), jnp.float32)

    def add(found, row, prod):
        pick = jnp.where(rowid == row, jnp.float32(1.0), jnp.float32(0.0))
        return found + lax.dot_general(pick, prod, (((1,), (1,)), ((), ())), precision=lax.Precision.HIGHEST,
                                       preferred_element_type=jnp.float32)

    for w in range(nslices):
        mw = xb[w].reshape(lq, 2 * nvec)
        for u in range(w + 1):
            mu = xb[u].reshape(lq, 2 * nvec)
            found = add(found, w * nslices + u, mw * mu)
            if u < w:
                found = add(found, u * nslices + w, mw * (pltpu.roll(mu, nvec, 1) * sign_r))
    ps[me] = jnp.zeros(ps.shape[1:], jnp.float32)
    ps[me, :, :lq] = found
    for o in range(1, nspace):
        p_copy(o).start()
    for o in range(1, nspace):
        p_copy(o).wait_recv()
    total = ps[0]
    for d in range(1, nspace):
        total = total + ps[d]
    lpad = total.shape[1]
    left_id = lax.broadcasted_iota(jnp.int32, (lpad, 128), 0)
    first = lax.broadcasted_iota(jnp.int32, (lpad, 128), 1) * rows
    fold = jnp.where((left_id >= first) & (left_id < first + rows), jnp.float32(1.0), jnp.float32(0.0))

    def exact_dot(p, r):
        return jnp.dot(p, r, precision=lax.Precision.HIGHEST, preferred_element_type=jnp.float32)

    table = exact_dot(total, fold) * jnp.float32(1.0 / nvec)
    source, sink = column(pair_ref, 0).astype(jnp.int32), column(pair_ref, 1).astype(jnp.int32)
    high, low = jnp.maximum(source, sink), jnp.minimum(source, sink)
    slot = lax.broadcasted_iota(jnp.int32, (pair_ref.shape[1], trows), 1)
    one, zero = jnp.float32(1.0), jnp.float32(0.0)
    turned = jnp.where(sink > source, one, jnp.where(sink < source, -one, zero))
    real = exact_dot(jnp.where(slot == high * nslices + low, one, zero), table)
    imag = exact_dot(jnp.where(slot == low * nslices + high, turned, zero), table)
    tr_ref[:, 0, :] = real[:, :moms]
    tr_ref[:, 1, :] = imag[:, :moms]

    for c in range(nchunks):
        core_copy(c).wait_send()
        y_copy(c).wait_send()
        for o in range(1, nz):
            z_copy(c, o).wait_send()
        for o in range(1, nslices):
            x_copy(c, o).wait_send()
    for o in range(1, nspace):
        p_copy(o).wait_send()


def local(solutions, noise, momenta, pairs):
    _, spincol, sites, width = solutions.shape
    nvec = width // 2
    moms = momenta.shape[0]
    nspace = lax.axis_size("space")
    nslices = lax.axis_size("tm")
    nz = nspace // 4
    rows = nvec // nspace
    nchunks = -(-moms // QC)
    scale = 1.0 / math.sqrt(spincol * sites * nspace)
    trows = -(-nslices * nslices // 8) * 8
    lq = nchunks * QC * rows
    lpad = -(-lq // 128) * 128
    dims = (nspace, nslices, nchunks, rows, nvec, spincol, scale)
    f32 = jnp.float32
    blk = (QC * rows, width)
    dma = pltpu.SemaphoreType.DMA
    vmem = pl.BlockSpec(memory_space=pltpu.VMEM)
    hbm = pl.BlockSpec(memory_space=pl.ANY)
    mesons, correlators = pl.pallas_call(
        functools.partial(kernel, dims),
        out_shape=(jax.ShapeDtypeStruct((2, moms, rows, nvec), f32),
                   jax.ShapeDtypeStruct((pairs.shape[0], 2, moms), f32)),
        in_specs=[vmem, vmem, hbm, hbm],
        out_specs=(vmem, vmem),
        scratch_shapes=[
            pltpu.VMEM((2, -(-nchunks * QC // 8) * 8, sites), f32),
            pltpu.VMEM((spincol, nvec, sites), jnp.int32),
            pltpu.VMEM((spincol, sites, width), jnp.bfloat16),
            pltpu.VMEM((spincol, nvec, sites), jnp.bfloat16),
            pltpu.VMEM((spincol, nvec, sites), jnp.bfloat16),
            pltpu.VMEM((2 * QC * nvec, width), f32),
            pltpu.VMEM((nchunks, 2, 2, nz) + blk, f32),
            pltpu.VMEM((nchunks, 2, nz) + blk, f32),
            pltpu.VMEM((nchunks, nz) + blk, f32),
            pltpu.VMEM((nchunks, 2, nz) + blk, f32),
            pltpu.VMEM((nchunks, nz) + blk, f32),
            pltpu.VMEM((nchunks, nz - 1) + blk, f32),
            pltpu.VMEM((nslices, nchunks) + blk, f32),
            pltpu.VMEM((nspace, trows, lpad), f32),
            dma((2,)),
            dma((nchunks,)), dma((nchunks,)),
            dma((nchunks,)), dma((nchunks,)),
            dma((nchunks, nz - 1)), dma((nchunks, nz - 1)),
            dma((nchunks, nslices - 1)), dma((nchunks, nslices - 1)),
            dma((nspace - 1,)), dma((nspace - 1,)),
        ],
        compiler_params=pltpu.CompilerParams(collective_id=0, has_side_effects=True, vmem_limit_bytes=60 * 2**20),
    )(momenta.T, pairs.T, noise[0].transpose(1, 0, 2), solutions[0])
    return (mesons[None], correlators)


def solution(mesh):
    in_specs = (P("tm", None, "space", None), P("tm", None, None, "space"), P(), P("tm", None))
    out_specs = (P("tm", None, None, "space", None), P("tm", None, None))
    return jax.shard_map(local, mesh=mesh, in_specs=in_specs, out_specs=out_specs, check_vma=False)
```

profile of v0, /device:TPU:0, one launch (start us, length us, event | category | flops | bytes accessed | tf_op | source)
XLA Modules:
  0.0 48.4 jit_solution(13348930596025271150)
XLA Ops:
  0.6 44.9 %shard_map.59 = (f32[2,27,4,64]{3,2,1,0:T(4,128)}, f32[8,2,27]{2,1,0:T(2,128)}) custom-call(s32[3,27]{1,0:T(4,128)} %bitcast.10, s32[2,8]{1,0:T(2,128)} %bitcast.11, s32[12,64,512]{2,1,0:T(8,128)} %bitcast.7, bf16[12,512,128]{2,1,0:T(8,128)(2,1)} %bitcast.8), custom_call_target="tpu_custom_call" | custom-call | tf_op jit(solution)/shard_map/pallas_call | solution.py:261
  45.6 1.5 %copy.8 = f32[1,2,27,4,64]{4,3,2,1,0:T(4,128)} copy(f32[1,2,27,4,64]{4,3,2,1,0:T(4,128)} %bitcast.9) | data formatting | bytes 110592
  47.1 1.3 %copy.9 = f32[8,2,27]{2,1,0:T(2,128)} copy(f32[8,2,27]{2,1,0:T(2,128)} %get-tuple-element.9) | data formatting | bytes 3456
where the time goes:
time: 48.6 us; the launch traced here: 48.4 us
  Pallas kernels  44.9 us (92%)
  local copies, waits for them, and re-layouts  2.84 us (6%)
  between operations  0.64 us (1%)
    pallas_call x1, Pallas kernels, local(): pl.pallas_call(functools.partial(kernel, dims), out_shape=(jax.ShapeDtype...  44.9 us
    unnamed x2, local copies, waits for them, and re-layouts  2.84 us

commit v1 on v0

v1 whole, which is shorter than its diff:
```python
import functools
import math

import jax
import jax.numpy as jnp
from jax import lax
from jax.experimental import pallas as pl
from jax.experimental.pallas import tpu as pltpu
from jax.sharding import PartitionSpec as P

EXTENT = 48
BLOCK = 64
LANES = 128
NCOMP = 5
HELD = (1.62322, 1.13025)
GAIN = (1.624206057120357, 1.1324218363011367)
MESH = pl.DeviceIdType.MESH
F32 = jnp.float32
BF16 = jnp.bfloat16


def fdiv(value, n):
    return jnp.floor((value + 0.5) * F32(1.0 / n))


def turn(value):
    return (value - fdiv(value, EXTENT) * EXTENT) * F32(2.0 * math.pi / EXTENT)


def iota(shape, axis):
    return lax.broadcasted_iota(jnp.int32, shape, axis)


def column(ref, row, size):
    line = jnp.broadcast_to(ref[row:row + 1, :size].astype(F32), (size, size))
    return jnp.sum(jnp.where(iota((size, size), 0) == iota((size, size), 1), line, F32(0.0)), axis=1, keepdims=True)


def coefficients(mom_ref, mp, offset, ngroup, kpad, scale):
    shape = (mp, kpad)
    lane = iota(shape, 1).astype(F32)
    part = fdiv(lane, ngroup)
    group = lane - part * ngroup
    rowslot = fdiv(group, NCOMP)
    comp = group - rowslot * NCOMP
    blk = fdiv(rowslot, 2)
    slot = rowslot - blk * 2
    row = fdiv(offset + blk * BLOCK, EXTENT) + slot
    zz = fdiv(row, EXTENT)
    yy = row - zz * EXTENT
    qx = jnp.broadcast_to(column(mom_ref, 0, mp), shape)
    qy = jnp.broadcast_to(column(mom_ref, 1, mp), shape)
    qz = jnp.broadcast_to(column(mom_ref, 2, mp), shape)
    angle = turn(qy * yy + qz * zz)
    c, s = jnp.cos(angle), jnp.sin(angle)
    side = jnp.where(qx < 0, F32(-1.0), F32(1.0))
    level = jnp.abs(qx)
    own = fdiv(comp + 1, 2)
    gain = jnp.where(own == 0, F32(scale), jnp.where(own == 1, F32(scale / GAIN[0]), F32(scale / GAIN[1])))
    gain = jnp.where((own == level) & (part < 3), gain, F32(0.0))
    is_sin = (comp == 2) | (comp == 4)
    a = jnp.where(is_sin, -side * s, c) * gain
    b = jnp.where(is_sin, side * c, s) * gain
    both = jnp.concatenate([a, b], axis=0)
    high = both.astype(BF16)
    low = (both - high.astype(F32)).astype(BF16)
    third = iota(both.shape, 1) >= 2 * ngroup
    return jnp.where(third, low.astype(F32), high.astype(F32)).astype(BF16)


def kernel(dims, mom_ref, pair_ref, noise_hbm, sol_hbm, mes_ref, tr_ref,
           raw, sol, momp, cmat, xtab, mask, field, sbuf, hbuf, qbuf, rcore, ry, rz, xb, ps,
           in_sem, cs, cr, ys, yr, zs, zr, xs, xr, pss, psr):
    nspace, nslices, rows, nvec, spincol, moms, scale = dims
    nz = nspace // 4
    ntile = raw.shape[0]
    nblk = ntile * 2
    ngroup = nblk * 2 * NCOMP
    mp = cmat.shape[0] // 2
    fs = nvec + 8
    me = lax.axis_index("space")
    slice_id = lax.axis_index("tm")
    core = lax.rem(me, 2)
    yy = lax.rem(me // 2, 2)
    zz = me // 4
    first = me * (ntile * LANES)

    barrier = pltpu.get_barrier_semaphore()
    for o in range(1, nspace):
        pl.semaphore_signal(barrier, inc=1, device_id={"space": lax.rem(me + o, nspace)}, device_id_type=MESH)
    for o in range(1, nslices):
        pl.semaphore_signal(barrier, inc=1, device_id={"tm": lax.rem(slice_id + o, nslices)}, device_id_type=MESH)

    def noise_copy(k):
        return pltpu.make_async_copy(noise_hbm.at[:, :, pl.ds(k * LANES, LANES)], raw.at[k], in_sem.at[0, k])

    def sol_copy(k):
        return pltpu.make_async_copy(sol_hbm.at[:, pl.ds(k * LANES, LANES), :], sol.at[k], in_sem.at[1, k])

    for k in range(ntile):
        noise_copy(k).start()
        sol_copy(k).start()

    offset = first.astype(F32)
    momp[...] = jnp.zeros_like(momp)
    momp[:3, :moms] = mom_ref[...].astype(F32)
    cmat[...] = coefficients(momp, mp, offset, ngroup, cmat.shape[1], scale)
    for blk in range(nblk):
        lane = iota((16, LANES), 1).astype(F32)
        site = lane - jnp.where(lane >= BLOCK, F32(BLOCK), F32(0.0))
        x = offset + F32(blk * BLOCK) + site
        for k in range(2):
            angle = turn(x * F32(k + 1))
            xtab[blk * 4 + 2 * k] = (jnp.cos(angle) * F32(HELD[k])).astype(BF16)
            xtab[blk * 4 + 2 * k + 1] = (jnp.sin(angle) * F32(HELD[k])).astype(BF16)
        t = iota((LANES, LANES), 0).astype(F32)
        t = t - jnp.where(t >= BLOCK, F32(BLOCK), F32(0.0))
        start = offset + F32(blk * BLOCK)
        mask[blk] = jnp.where(fdiv(start + t, EXTENT) == fdiv(start, EXTENT), F32(1.0), F32(0.0)).astype(BF16)

    low = iota((nvec, LANES), 1) < BLOCK
    rsign = jnp.where(iota((LANES, LANES), 1) < nvec, F32(-1.0), F32(1.0)).astype(BF16)

    def spread(v, n):
        return jnp.concatenate([v] * n, axis=0)

    for k in range(ntile):
        noise_copy(k).wait()
        sol_copy(k).wait()
        for h in range(2):
            blk = 2 * k + h
            xs_rows = [spread(xtab[blk * 4 + c], nvec // 16) for c in range(4)]
            keep = mask[blk]
            total = None
            for p in range(spincol // 2):
                ka = raw[k, 2 * p]
                kb = raw[k, 2 * p + 1]
                if h == 0:
                    kk = jnp.where(low, ka, pltpu.roll(kb, BLOCK, 1))
                else:
                    kk = jnp.where(low, pltpu.roll(ka, BLOCK, 1), kb)
                kf = kk.astype(F32)
                re = jnp.where(kk == 3, F32(0.0), F32(1.0) - kf).astype(BF16)
                im = jnp.where(kk == 0, F32(0.0), kf - F32(2.0)).astype(BF16)
                parts = [jnp.concatenate([re, im], axis=1)]
                for c in range(4):
                    parts.append(jnp.concatenate([re * xs_rows[c], im * xs_rows[c]], axis=1))
                lhs = jnp.concatenate(parts, axis=0)
                v = jnp.concatenate([sol[k, 2 * p, h * BLOCK:(h + 1) * BLOCK, :],
                                     sol[k, 2 * p + 1, h * BLOCK:(h + 1) * BLOCK, :]], axis=0)
                rv = pltpu.roll(v, nvec, 1) * rsign
                v0, rv0 = v * keep, rv * keep
                rhs = jnp.concatenate([jnp.concatenate([v0, v - v0], axis=1),
                                       jnp.concatenate([rv0, rv - rv0], axis=1)], axis=0)
                prod = jnp.dot(lhs, rhs, preferred_element_type=F32)
                total = prod if total is None else total + prod
            for slot in range(2):
                for c in range(NCOMP):
                    g = (blk * 2 + slot) * NCOMP + c
                    field[g * fs:g * fs + nvec, :] = total[c * nvec:(c + 1) * nvec, slot * LANES:(slot + 1) * LANES]

    def remote(src, dst, ssem, rsem, where):
        return pltpu.make_async_remote_copy(src_ref=src, dst_ref=dst, send_sem=ssem, recv_sem=rsem,
                                            device_id=where, device_id_type=MESH)

    used = pl.ds(0, moms)

    def peer(m):
        if nz & (nz - 1):
            return lax.rem(zz + m, nz)
        out, bit = 0, 1
        while bit < nz:
            digit = lax.rem(zz // bit, 2)
            out = out + bit * (1 - digit if m & bit else digit)
            bit *= 2
        return out

    core_peer = {"space": me + 1 - 2 * core}
    y_peer = {"space": me + 2 - 4 * yy}
    order = list(range(nz - 1, -1, -1))

    def core_copy(m, far):
        return remote(sbuf.at[far, m, 1 - core, :, used], rcore.at[far, m, :, used], cs.at[far, m], cr.at[far, m],
                      core_peer)

    def y_copy(m):
        return remote(hbuf.at[m, :, used], ry.at[m, :, used], ys.at[m], yr.at[m], y_peer)

    def z_copy(m):
        return remote(qbuf.at[m, :, used], rz.at[m, :, used], zs.at[m], zr.at[m],
                      {"space": peer(m) * 4 + yy * 2 + core})

    def x_copy(o):
        return remote(xb.at[slice_id, :, used], xb.at[slice_id, :, used], xs.at[o - 1], xr.at[o - 1],
                      {"tm": lax.rem(slice_id + o, nslices)})

    def p_copy(o):
        return remote(ps.at[me], ps.at[me], pss.at[o - 1], psr.at[o - 1],
                      {"space": lax.rem(me + o, nspace)})

    osign = jnp.where(iota((mp, LANES), 1) < nvec, F32(1.0), F32(-1.0))
    kpad = cmat.shape[1]

    def compute(m, far):
        base = peer(m) * (4 * rows) + (1 - yy if far else yy) * (2 * rows)
        coef = cmat[...]
        for pair in range(rows):
            xf = jnp.concatenate([field[pl.ds(base + 2 * pair + e, ngroup, stride=fs), :] for e in range(2)], axis=1)
            high = xf.astype(BF16)
            rest = (xf - high.astype(F32)).astype(BF16)
            stack = [high, rest, high]
            if kpad > 3 * ngroup:
                stack.append(jnp.zeros((kpad - 3 * ngroup, 2 * LANES), BF16))
            res = jnp.dot(coef, jnp.concatenate(stack, axis=0), preferred_element_type=F32)
            for e in range(2):
                idx = 2 * pair + e
                a = res[:mp, e * LANES:(e + 1) * LANES]
                b = res[mp:, e * LANES:(e + 1) * LANES]
                sbuf[far, m, idx // rows, idx % rows] = a + pltpu.roll(b, nvec, 1) * osign

    started = False
    for far in (1, 0):
        for m in order:
            compute(m, far)
            if not started:
                pl.semaphore_wait(barrier, nspace - 1 + nslices - 1)
                started = True
            core_copy(m, far).start()

    for m in order:
        core_copy(m, 1).wait_recv()
        hbuf[m] = sbuf[1, m, core] + rcore[1, m]
        y_copy(m).start()
    for m in order[:-1]:
        core_copy(m, 0).wait_recv()
        y_copy(m).wait_recv()
        qbuf[m] = (sbuf[0, m, core] + rcore[0, m]) + ry[m]
        z_copy(m).start()
    core_copy(0, 0).wait_recv()
    y_copy(0).wait_recv()
    total = (sbuf[0, 0, core] + rcore[0, 0]) + ry[0]
    for m in order[:-1]:
        z_copy(m).wait_recv()
        total = total + rz[m]
    xb[slice_id] = total
    for o in range(1, nslices):
        x_copy(o).start()
    for r in range(rows):
        mes_ref[0, r] = total[r, :moms, :nvec]
        mes_ref[1, r] = pltpu.roll(total[r], nvec, 1)[:moms, :nvec]
    for o in range(1, nslices):
        x_copy(o).wait_recv()

    prods = [None] * (nslices * nslices)
    for w in range(nslices):
        for u in range(w + 1):
            re = im = None
            for r in range(rows):
                mw, mu = xb[w, r], xb[u, r]
                part = mw * mu
                re = part if re is None else re + part
                if u < w:
                    part = mw * (pltpu.roll(mu, nvec, 1) * osign)
                    im = part if im is None else im + part
            prods[w * nslices + u] = re
            if u < w:
                prods[u * nslices + w] = -im
    table = jnp.concatenate(prods, axis=0)
    found = lax.dot_general(jnp.ones((8, LANES), F32), table, (((1,), (1,)), ((), ())),
                            precision=lax.Precision.HIGHEST, preferred_element_type=F32)
    ps[me] = found[0:1]
    for o in range(1, nspace):
        p_copy(o).start()
    for o in range(1, nspace):
        p_copy(o).wait_recv()
    tot = ps[0]
    for d in range(1, nspace):
        tot = tot + ps[d]
    tot = tot * F32(1.0 / nvec)
    npair = pair_ref.shape[1]
    source, sink = column(pair_ref, 0, npair), column(pair_ref, 1, npair)
    high, small = jnp.maximum(source, sink), jnp.minimum(source, sink)
    turned = jnp.where(sink > source, F32(1.0), jnp.where(sink < source, F32(-1.0), F32(0.0)))
    real = jnp.zeros((npair, mp), F32)
    imag = jnp.zeros((npair, mp), F32)
    for k in range(nslices * nslices):
        line = tot[:, k * mp:(k + 1) * mp]
        real = real + jnp.where(high * nslices + small == k, F32(1.0), F32(0.0)) * line
        imag = imag + jnp.where(small * nslices + high == k, turned, F32(0.0)) * line
    tr_ref[:, 0, :] = real[:, :moms]
    tr_ref[:, 1, :] = imag[:, :moms]

    for m in order:
        core_copy(m, 0).wait_send()
        core_copy(m, 1).wait_send()
        y_copy(m).wait_send()
    for m in order[:-1]:
        z_copy(m).wait_send()
    for o in range(1, nslices):
        x_copy(o).wait_send()
    for o in range(1, nspace):
        p_copy(o).wait_send()


def local(solutions, noise, momenta, pairs):
    _, spincol, sites, width = solutions.shape
    nvec = width // 2
    moms = momenta.shape[0]
    nspace = lax.axis_size("space")
    nslices = lax.axis_size("tm")
    nz = nspace // 4
    rows = nvec // nspace
    scale = 1.0 / math.sqrt(spincol * sites * nspace)
    ntile = sites // LANES
    ngroup = ntile * 4 * NCOMP
    kpad = -(-3 * ngroup // LANES) * LANES
    mp = -(-moms // 16) * 16
    blk = (rows, mp, width)
    dims = (nspace, nslices, rows, nvec, spincol, moms, scale)
    dma = pltpu.SemaphoreType.DMA
    vmem = pl.BlockSpec(memory_space=pltpu.VMEM)
    hbm = pl.BlockSpec(memory_space=pl.ANY)
    mesons, correlators = pl.pallas_call(
        functools.partial(kernel, dims),
        out_shape=(jax.ShapeDtypeStruct((2, rows, moms, nvec), F32),
                   jax.ShapeDtypeStruct((pairs.shape[0], 2, moms), F32)),
        in_specs=[vmem, vmem, hbm, hbm],
        out_specs=(vmem, vmem),
        scratch_shapes=[
            pltpu.VMEM((ntile, spincol, nvec, LANES), jnp.int32),
            pltpu.VMEM((ntile, spincol, LANES, width), BF16),
            pltpu.VMEM((8, -(-mp // LANES) * LANES), F32),
            pltpu.VMEM((2 * mp, kpad), BF16),
            pltpu.VMEM((ntile * 8, 16, LANES), BF16),
            pltpu.VMEM((ntile * 2, LANES, LANES), BF16),
            pltpu.VMEM((ngroup * (nvec + 8), width), F32),
            pltpu.VMEM((2, nz, 2) + blk, F32),
            pltpu.VMEM((nz,) + blk, F32),
            pltpu.VMEM((nz,) + blk, F32),
            pltpu.VMEM((2, nz) + blk, F32),
            pltpu.VMEM((nz,) + blk, F32),
            pltpu.VMEM((nz,) + blk, F32),
            pltpu.VMEM((nslices,) + blk, F32),
            pltpu.VMEM((nspace, 1, nslices * nslices * mp), F32),
            dma((2, ntile)),
            dma((2, nz)), dma((2, nz)),
            dma((nz,)), dma((nz,)),
            dma((nz,)), dma((nz,)),
            dma((nslices - 1,)), dma((nslices - 1,)),
            dma((nspace - 1,)), dma((nspace - 1,)),
        ],
        compiler_params=pltpu.CompilerParams(collective_id=0, has_side_effects=True, vmem_limit_bytes=60 * 2**20),
    )(momenta.T, pairs.T, noise[0].transpose(1, 0, 2), solutions[0])
    return (mesons.transpose(0, 2, 1, 3)[None], correlators)


def solution(mesh):
    in_specs = (P("tm", None, "space", None), P("tm", None, None, "space"), P(), P("tm", None))
    out_specs = (P("tm", None, None, "space", None), P("tm", None, None))
    return jax.shard_map(local, mesh=mesh, in_specs=in_specs, out_specs=out_specs, check_vma=False)
```

time: 48.6 us -> 32.4 us (0.67)
  Pallas kernels: 44.9 us -> 28.6 us
    pallas_call x1, Pallas kernels: 44.9 us -> 28.6 us  [local(): pl.pallas_call(functools.partial(kernel, dims), out_shape=(jax.ShapeDtype...]
where the time goes in v1:
time: 32.4 us; the launch traced here: 32.1 us
  Pallas kernels  28.6 us (88%)
  local copies, waits for them, and re-layouts  2.92 us (9%)
  between operations  0.64 us (2%)
    pallas_call x1, Pallas kernels, local(): pl.pallas_call(functools.partial(kernel, dims), out_shape=(jax.ShapeDtype...  28.6 us
    unnamed x2, local copies, waits for them, and re-layouts  2.92 us

profile of v1, /device:TPU:0, one launch (start us, length us, event | category | flops | bytes accessed | tf_op | source)
XLA Modules:
  0.0 32.1 jit_solution(2778662046343525018)
XLA Ops:
  0.6 28.6 %shard_map.59 = (f32[2,4,27,64]{3,2,1,0:T(8,128)}, f32[8,2,27]{2,1,0:T(2,128)}) custom-call(s32[3,27]{1,0:T(4,128)} %bitcast.12, s32[2,8]{1,0:T(2,128)} %bitcast.13, s32[12,64,512]{2,1,0:T(8,128)} %bitcast.9, bf16[12,512,128]{2,1,0:T(8,128)(2,1)} %bitcast.10), custom_call_target="tpu_custom_call" | custom-call | tf_op jit(solution)/shard_map/pallas_call | solution.py:323
  29.2 1.6 %copy.6 = f32[1,2,27,4,64]{4,3,2,1,0:T(4,128)} copy(f32[1,2,27,4,64]{4,2,3,1,0:T(8,128)} %bitcast.11) | data formatting | bytes 110592
  30.8 1.3 %copy.8 = f32[8,2,27]{2,1,0:T(2,128)} copy(f32[8,2,27]{2,1,0:T(2,128)} %get-tuple-element.11) | data formatting | bytes 3456
